TPU v7x, 32 devices: a whole 2x2x4 slice. The times are simulated.
32 devices in a mesh: row: 4 (over y, x), col: 8 (over z, core).
Axes of the slice: x: 2, y: 2, z: 4, core: 2. Of those that a mesh axis runs over, the one named last changes fastest.
Arguments:
- amplitudes: bfloat16 [800, 800, 768], P('row', 'col'), may hold values from -6 to 6
- integrals: bfloat16 [800, 800, 256], P('row', 'col'), may hold values from -0.375 to 0.375
- window_index: int32 [256], replicated, may hold values from 0 to 639999, as said below
Outputs:
- residual: bfloat16 [800, 800, 768], P('row', 'col')
- pair_energy: float32 [768], replicated
Inputs may be any that keep to these rules, and one draw needn't show every extreme that they name: `window_index`: the window pairs are distinct; pair k lies in the block of a rows and b columns owned by device number k // 8 in row-major order of the (a, b) device grid, 8 pairs for each block.
All inputs are finite; a program needn't handle non-finite values.
Results may differ from a plain program's by a relative error of at most 0.001.
Values may be sent and summed in bfloat16 or wider, within the bound.
A program may use at most 256 MiB of HBM per device.

v0:
```python
import jax
import jax.numpy as jnp
from jax import lax
from jax.sharding import PartitionSpec as P


def shards(amplitudes, integrals, window_index):
    block_rows, block_cols, pairs = amplitudes.shape
    window = integrals.shape[2]
    ncols = lax.axis_size("col")
    nrows = lax.axis_size("row")
    per_device = window // (nrows * ncols)
    row_rank = lax.axis_index("row")
    col_rank = lax.axis_index("col")
    linear_rank = row_rank * ncols + col_rank
    owned_index = lax.dynamic_slice_in_dim(window_index, linear_rank * per_device, per_device)
    virtuals = block_rows * nrows
    row_offset = owned_index // virtuals - row_rank * block_rows
    col_offset = owned_index % virtuals - col_rank * block_cols
    owned = amplitudes[row_offset, col_offset]
    in_row = lax.all_gather(owned, "col", axis=0, tiled=True)
    columns = lax.all_gather(in_row, "row", axis=0, tiled=True)
    full = jnp.einsum("abk,kp->abp", integrals, columns, preferred_element_type=jnp.float32)
    partial_value = jnp.sum(amplitudes.astype(jnp.float32) * full, axis=(0, 1))
    pair_energy = lax.psum(partial_value, ("row", "col")) / virtuals
    residual = full.astype(jnp.bfloat16)
    return (residual, pair_energy)


def solution(mesh):
    return jax.shard_map(
        shards,
        mesh=mesh,
        in_specs=(P("row", "col", None), P("row", "col", None), P()),
        out_specs=(P("row", "col", None), P()),
        check_vma=False,
    )
```

profile of v0, /device:TPU:0, one launch (start us, length us, event | category | flops | bytes accessed | tf_op | source)
XLA Modules:
  0.0 172.8 jit_solution(1093921430304254708)
XLA Ops:
  0.6 0.8 fusion.7
  1.4 1.4 gather_fusion
  2.8 15.6 %all_gather.6 = bf16[64,768]{1,0:T(8,128)(2,1)S(1)} all-gather(bf16[8,768]{1,0:T(8,128)(2,1)S(1)} %gather_fusion), channel_id=1, replica_groups=mesh['row'=4,'col'=8] {'col'}, dimensions={0}, use_global_device_ids=true | all-gather | bytes 110592 | tf_op jit(solution)/shard_map/all_gather | solution.py:21
  18.4 9.5 %all_gather.7 = bf16[256,768]{1,0:T(8,128)(2,1)S(1)} all-gather(bf16[64,768]{1,0:T(8,128)(2,1)S(1)} %all_gather.6), channel_id=1, replica_groups=mesh['row'=4,'col'=8] {'row'}, dimensions={0}, use_global_device_ids=true | all-gather | bytes 491520 | tf_op jit(solution)/shard_map/all_gather | solution.py:22
  27.9 44.0 %bitcast_convert_fusion = (bf16[200,100,768]{2,1,0:T(8,128)(2,1)}, f32[768,200,100]{0,2,1:T(8,128)}) fusion(bf16[200,100,256]{2,0,1:T(8,128)(2,1)} %param.4, bf16[256,768]{1,0:T(8,128)(2,1)S(1)} %all_gather.7), kind=kOutput, calls=%fused_computation.2 | convolution fusion | flops 7879680000 | bytes 102793216 | tf_op jit(solution)/shard_map/abk,kp->abp/dot_general | solution.py:23
  71.9 22.0 %copy.7 = bf16[200,100,768]{2,0,1:T(8,128)(2,1)} copy(bf16[200,100,768]{2,1,0:T(8,128)(2,1)} %get-tuple-element.4) | data formatting | bytes 61440000
  93.9 39.0 %fusion = f32[768]{0:T(1024)S(1)} fusion(f32[768,200,100]{0,2,1:T(8,128)} %get-tuple-element.5, bf16[200,100,768]{2,0,1:T(8,128)(2,1)} %param.3), kind=kLoop, calls=%fused_computation.3 | loop fusion | flops 46079232 | bytes 92163072 | tf_op jit(solution)/shard_map/reduce_sum | solution.py:24
  132.9 39.3 %psum.7 = f32[768]{0:T(1024)S(1)} all-reduce(f32[768]{0:T(1024)S(1)} %fusion), channel_id=1, replica_groups=mesh['row'=4,'col'=8] {'row','col'}, use_global_device_ids=true, to_apply=%region_1.2 | all-reduce | flops 768 | bytes 6144 | tf_op jit(solution)/shard_map/psum | solution.py:25
  172.2 0.6 broadcast_multiply_fusion
where the time goes:
time: 173 us
  blocking collectives  64.5 us (37%)
  matrix products  44 us (25%)
  other arithmetic  40.3 us (23%)
  local copies, waits for them, and re-layouts  23.3 us (13%)
    dot_general x1, matrix products, shards(): jnp.einsum('abk,kp->abp', integrals, columns, preferred_element_type=jnp....  44 us
    psum x1, blocking collectives, shards(): pair_energy = lax.psum(partial_value, ('row', 'col')) / virtuals  39.3 us
    reduce_sum x1, other arithmetic, shards(): partial_value = jnp.sum(amplitudes.astype(jnp.float32) * full, axis=(0, 1))  39 us
    unnamed x1, local copies, waits for them, and re-layouts  22 us
    all_gather x1, blocking collectives, shards(): in_row = lax.all_gather(owned, 'col', axis=0, tiled=True)  15.6 us
    all_gather x1, blocking collectives, shards(): columns = lax.all_gather(in_row, 'row', axis=0, tiled=True)  9.5 us

commit v1 on v0

--- a/solution.py
+++ b/solution.py
@@ -18,7 +18,20 @@
     row_offset = owned_index // virtuals - row_rank * block_rows
     col_offset = owned_index % virtuals - col_rank * block_cols
     owned = amplitudes[row_offset, col_offset]
-    in_row = lax.all_gather(owned, "col", axis=0, tiled=True)
+
+    def switch_page_for(u_in):
+        mesh_ax = "col"
+        full_n = lax.axis_size(mesh_ax)
+        row_list = [u_in]
+        for idx in range(full_n - 1):
+            current_arr = lax.ppermute(
+                row_list[-1], mesh_ax, [(k0, (k0 + 1) % full_n) for k0 in range(full_n)]
+            )
+            row_list.append(current_arr)
+        base_arr = jnp.concatenate(row_list[::-1], axis=0)
+        return jnp.roll(base_arr, (lax.axis_index(mesh_ax) + 1) * u_in.shape[0], axis=0)
+
+    in_row = switch_page_for(owned)
     columns = lax.all_gather(in_row, "row", axis=0, tiled=True)
     full = jnp.einsum("abk,kp->abp", integrals, columns, preferred_element_type=jnp.float32)
     partial_value = jnp.sum(amplitudes.astype(jnp.float32) * full, axis=(0, 1))

time: 173 us -> 192 us (1.11)
  waiting for transfers between devices: 0 us -> 34.9 us
  blocking collectives: 64.5 us -> 46.9 us
    ppermute x0 -> x7, waiting for transfers between devices: none -> 34.9 us  [switch_page_for(): lax.ppermute(row_list[-1], mesh_ax, [(k0, (k0 + 1) % full_n) for k0 in ra...]
    all_gather x1 -> x0, blocking collectives: 15.6 us -> none  [shards(): in_row = lax.all_gather(owned, 'col', axis=0, tiled=True)]
    psum x1, blocking collectives: 39.3 us -> 36.9 us  [shards(): pair_energy = lax.psum(partial_value, ('row', 'col')) / virtuals]
    unnamed x1 -> x16, local copies, waits for them, and re-layouts: 22 us -> 22 us
  transfers between devices with their start and end apart: 0 -> 7, of which waited for: 0 -> 7; matrix products, arithmetic and copies ran while one was open for 0% -> 0% of each run, Pallas kernels for 0% -> 0%
where the time goes in v1:
time: 192 us; the launch traced here: 191 us
  blocking collectives  46.9 us (24%)
  matrix products  44.1 us (23%)
  other arithmetic  40.3 us (21%)
  waiting for transfers between devices  34.9 us (18%)
  local copies, waits for them, and re-layouts  23.4 us (12%)
    dot_general x1, matrix products, shards(): jnp.einsum('abk,kp->abp', integrals, columns, preferred_element_type=jnp....  44.1 us
    reduce_sum x1, other arithmetic, shards(): partial_value = jnp.sum(amplitudes.astype(jnp.float32) * full, axis=(0, 1))  39 us
    psum x1, blocking collectives, shards(): pair_energy = lax.psum(partial_value, ('row', 'col')) / virtuals  36.9 us
    ppermute x7, waiting for transfers between devices, switch_page_for(): lax.ppermute(row_list[-1], mesh_ax, [(k0, (k0 + 1) % full_n) for k0 in ra...  34.9 us
    unnamed x16, local copies, waits for them, and re-layouts  22 us
    all_gather x1, blocking collectives, shards(): columns = lax.all_gather(in_row, 'row', axis=0, tiled=True)  10 us
  transfers between devices with their start and end apart: 7, of which 7 were waited for; matrix products, arithmetic and copies ran while one was open for 0% of the time, Pallas kernels for 0%

profile of v1, /device:TPU:0, one launch (start us, length us, event | category | flops | bytes accessed | tf_op | source)
XLA Modules:
  0.0 190.9 jit_solution(15600632935285199421)
XLA Ops:
  0.6 0.8 fusion.7
  1.4 1.4 gather_fusion
  2.8 0.5 collective-permute-start
  3.3 5.4 %collective-permute-done = bf16[8,768]{1,0:T(8,128)(2,1)S(1)} collective-permute-done((bf16[8,768]{1,0:T(8,128)(2,1)S(1)}, bf16[8,768]{1,0:T(8,128)(2,1)S(1)}, u32[]{:S(2)}, u32[]{:S(2)}) %collective-permute-start) | collective-permute-done | bytes 12320 | tf_op jit(solution)/shard_map/ppermute | solution.py:27
  8.7 0.0 collective-permute-start.1
  8.7 4.9 %collective-permute-done.1 = bf16[8,768]{1,0:T(8,128)(2,1)S(1)} collective-permute-done((bf16[8,768]{1,0:T(8,128)(2,1)S(1)}, bf16[8,768]{1,0:T(8,128)(2,1)S(1)}, u32[]{:S(2)}, u32[]{:S(2)}) %collective-permute-start.1) | collective-permute-done | bytes 12320 | tf_op jit(solution)/shard_map/ppermute | solution.py:27
  13.7 0.0 collective-permute-start.2
  13.7 4.9 %collective-permute-done.2 = bf16[8,768]{1,0:T(8,128)(2,1)S(1)} collective-permute-done((bf16[8,768]{1,0:T(8,128)(2,1)S(1)}, bf16[8,768]{1,0:T(8,128)(2,1)S(1)}, u32[]{:S(2)}, u32[]{:S(2)}) %collective-permute-start.2) | collective-permute-done | bytes 12320 | tf_op jit(solution)/shard_map/ppermute | solution.py:27
  18.6 0.0 collective-permute-start.3
  18.6 4.9 %collective-permute-done.3 = bf16[8,768]{1,0:T(8,128)(2,1)S(1)} collective-permute-done((bf16[8,768]{1,0:T(8,128)(2,1)S(1)}, bf16[8,768]{1,0:T(8,128)(2,1)S(1)}, u32[]{:S(2)}, u32[]{:S(2)}) %collective-permute-start.3) | collective-permute-done | bytes 12320 | tf_op jit(solution)/shard_map/ppermute | solution.py:27
  23.5 0.0 collective-permute-start.4
  23.5 4.9 %collective-permute-done.4 = bf16[8,768]{1,0:T(8,128)(2,1)S(1)} collective-permute-done((bf16[8,768]{1,0:T(8,128)(2,1)S(1)}, bf16[8,768]{1,0:T(8,128)(2,1)S(1)}, u32[]{:S(2)}, u32[]{:S(2)}) %collective-permute-start.4) | collective-permute-done | bytes 12320 | tf_op jit(solution)/shard_map/ppermute | solution.py:27
  28.4 0.0 collective-permute-start.5
  28.4 4.9 %collective-permute-done.5 = bf16[8,768]{1,0:T(8,128)(2,1)S(1)} collective-permute-done((bf16[8,768]{1,0:T(8,128)(2,1)S(1)}, bf16[8,768]{1,0:T(8,128)(2,1)S(1)}, u32[]{:S(2)}, u32[]{:S(2)}) %collective-permute-start.5) | collective-permute-done | bytes 12320 | tf_op jit(solution)/shard_map/ppermute | solution.py:27
  33.3 0.0 collective-permute-start.6
  33.3 4.9 %collective-permute-done.6 = bf16[8,768]{1,0:T(8,128)(2,1)S(1)} collective-permute-done((bf16[8,768]{1,0:T(8,128)(2,1)S(1)}, bf16[8,768]{1,0:T(8,128)(2,1)S(1)}, u32[]{:S(2)}, u32[]{:S(2)}) %collective-permute-start.6) | collective-permute-done | bytes 12320 | tf_op jit(solution)/shard_map/ppermute | solution.py:27
  38.4 10.0 %all_gather.3 = bf16[256,768]{1,0:T(8,128)(2,1)S(1)} all-gather(bf16[64,768]{1,0:T(8,128)(2,1)S(1)} %constant_dynamic-slice_fusion), channel_id=1, replica_groups=mesh['row'=4,'col'=8] {'row'}, dimensions={0}, use_global_device_ids=true | all-gather | bytes 491520 | tf_op jit(solution)/shard_map/all_gather | solution.py:35
  48.4 44.1 %bitcast_convert_fusion = (bf16[200,100,768]{2,1,0:T(8,128)(2,1)}, f32[768,200,100]{0,2,1:T(8,128)}) fusion(bf16[200,100,256]{2,0,1:T(8,128)(2,1)} %param.4, bf16[256,768]{1,0:T(8,128)(2,1)S(1)} %all_gather.3), kind=kOutput, calls=%fused_computation.2 | convolution fusion | flops 7879680000 | bytes 102793216 | tf_op jit(solution)/shard_map/abk,kp->abp/dot_general | solution.py:36
  92.5 22.0 %copy.7 = bf16[200,100,768]{2,0,1:T(8,128)(2,1)} copy(bf16[200,100,768]{2,1,0:T(8,128)(2,1)} %get-tuple-element.4) | data formatting | bytes 61440000
  114.5 39.0 %fusion = f32[768]{0:T(1024)S(1)} fusion(f32[768,200,100]{0,2,1:T(8,128)} %get-tuple-element.5, bf16[200,100,768]{2,0,1:T(8,128)(2,1)} %param.3), kind=kLoop, calls=%fused_computation.3 | loop fusion | flops 46079232 | bytes 92163072 | tf_op jit(solution)/shard_map/reduce_sum | solution.py:37
  153.4 36.9 %psum.7 = f32[768]{0:T(1024)S(1)} all-reduce(f32[768]{0:T(1024)S(1)} %fusion), channel_id=1, replica_groups=mesh['row'=4,'col'=8] {'row','col'}, use_global_device_ids=true, to_apply=%region_1.2 | all-reduce | flops 768 | bytes 6144 | tf_op jit(solution)/shard_map/psum | solution.py:38
  190.3 0.6 broadcast_multiply_fusion
  (17 shorter events, 0.1 us)
Async XLA Ops:
  2.8 5.9 %collective-permute-start = (bf16[8,768]{1,0:T(8,128)(2,1)S(1)}, bf16[8,768]{1,0:T(8,128)(2,1)S(1)}, u32[]{:S(2)}, u32[]{:S(2)}) collective-permute-start(bf16[8,768]{1,0:T(8,128)(2,1)S(1)} %gather_fusion), channel_id=1, source_target_pairs={{0,1},{1,2},{2,3},{3,4},{4,5},{5,6},{6,7},{7,0},{8,9},{9,10},{10,1... | collective-permute-start | bytes 36872 | tf_op jit(solution)/shard_map/ppermute | solution.py:27
  8.7 4.9 %collective-permute-start.1 = (bf16[8,768]{1,0:T(8,128)(2,1)S(1)}, bf16[8,768]{1,0:T(8,128)(2,1)S(1)}, u32[]{:S(2)}, u32[]{:S(2)}) collective-permute-start(bf16[8,768]{1,0:T(8,128)(2,1)S(1)} %collective-permute-done), channel_id=1, source_target_pairs={{0,1},{1,2},{2,3},{3,4},{4,5},{5,6},{6,7},{7,0},{8,9},{9,10},{10,1... | collective-permute-start | bytes 36872 | tf_op jit(solution)/shard_map/ppermute | solution.py:27
  13.7 4.9 %collective-permute-start.2 = (bf16[8,768]{1,0:T(8,128)(2,1)S(1)}, bf16[8,768]{1,0:T(8,128)(2,1)S(1)}, u32[]{:S(2)}, u32[]{:S(2)}) collective-permute-start(bf16[8,768]{1,0:T(8,128)(2,1)S(1)} %collective-permute-done.1), channel_id=1, source_target_pairs={{0,1},{1,2},{2,3},{3,4},{4,5},{5,6},{6,7},{7,0},{8,9},{9,10},{10,1... | collective-permute-start | bytes 36872 | tf_op jit(solution)/shard_map/ppermute | solution.py:27
  18.6 4.9 %collective-permute-start.3 = (bf16[8,768]{1,0:T(8,128)(2,1)S(1)}, bf16[8,768]{1,0:T(8,128)(2,1)S(1)}, u32[]{:S(2)}, u32[]{:S(2)}) collective-permute-start(bf16[8,768]{1,0:T(8,128)(2,1)S(1)} %collective-permute-done.2), channel_id=1, source_target_pairs={{0,1},{1,2},{2,3},{3,4},{4,5},{5,6},{6,7},{7,0},{8,9},{9,10},{10,1... | collective-permute-start | bytes 36872 | tf_op jit(solution)/shard_map/ppermute | solution.py:27
  23.5 4.9 %collective-permute-start.4 = (bf16[8,768]{1,0:T(8,128)(2,1)S(1)}, bf16[8,768]{1,0:T(8,128)(2,1)S(1)}, u32[]{:S(2)}, u32[]{:S(2)}) collective-permute-start(bf16[8,768]{1,0:T(8,128)(2,1)S(1)} %collective-permute-done.3), channel_id=1, source_target_pairs={{0,1},{1,2},{2,3},{3,4},{4,5},{5,6},{6,7},{7,0},{8,9},{9,10},{10,1... | collective-permute-start | bytes 36872 | tf_op jit(solution)/shard_map/ppermute | solution.py:27
  28.4 4.9 %collective-permute-start.5 = (bf16[8,768]{1,0:T(8,128)(2,1)S(1)}, bf16[8,768]{1,0:T(8,128)(2,1)S(1)}, u32[]{:S(2)}, u32[]{:S(2)}) collective-permute-start(bf16[8,768]{1,0:T(8,128)(2,1)S(1)} %collective-permute-done.4), channel_id=1, source_target_pairs={{0,1},{1,2},{2,3},{3,4},{4,5},{5,6},{6,7},{7,0},{8,9},{9,10},{10,1... | collective-permute-start | bytes 36872 | tf_op jit(solution)/shard_map/ppermute | solution.py:27
  33.3 4.9 %collective-permute-start.6 = (bf16[8,768]{1,0:T(8,128)(2,1)S(1)}, bf16[8,768]{1,0:T(8,128)(2,1)S(1)}, u32[]{:S(2)}, u32[]{:S(2)}) collective-permute-start(bf16[8,768]{1,0:T(8,128)(2,1)S(1)} %collective-permute-done.5), channel_id=1, source_target_pairs={{0,1},{1,2},{2,3},{3,4},{4,5},{5,6},{6,7},{7,0},{8,9},{9,10},{10,1... | collective-permute-start | bytes 36872 | tf_op jit(solution)/shard_map/ppermute | solution.py:27
